TPU v7x, 32 devices: a 4x4x1 block of a 4x4x8 slice. The times are simulated.
32 devices in a mesh: dp: 1 (over z), sp: 4 (over y), tp: 8 (over x, core).
Axes of the slice: x: 4, y: 4, z: 1, core: 2. Of those that a mesh axis runs over, the one named last changes fastest.
The devices are a block of a 4x4x8 slice.
Arguments:
- x_in: bfloat16 [128, 4096], P('dp')
- lengths: int32 [128], P('dp')
- w_q: bfloat16 [2, 4096, 4096], P(None, None, 'tp')
- w_k: bfloat16 [2, 4096, 1024], P(None, None, 'tp')
- w_v: bfloat16 [2, 4096, 1024], P(None, None, 'tp')
- w_o: bfloat16 [2, 4096, 4096], P(None, 'tp')
- w_gate: bfloat16 [2, 4096, 14336], P(None, None, 'tp')
- w_up: bfloat16 [2, 4096, 14336], P(None, None, 'tp')
- w_down: bfloat16 [2, 14336, 4096], P(None, 'tp')
- gain_attn: bfloat16 [2, 4096], replicated
- gain_mlp: bfloat16 [2, 4096], replicated
- k_cache: bfloat16 [2, 128, 8, 256, 128], P(None, 'dp', 'tp', 'sp')
- v_cache: bfloat16 [2, 128, 8, 256, 128], P(None, 'dp', 'tp', 'sp')
Outputs:
- output 1: bfloat16 [128, 4096], P('dp')
- output 2: bfloat16 [2, 128, 8, 128], P(None, 'dp', 'tp')
- output 3: bfloat16 [2, 128, 8, 128], P(None, 'dp', 'tp')
All inputs are finite; a program needn't handle non-finite values.
Results may differ from a plain program's by a relative error of at most 0.02.
Values are sent between devices in bfloat16 or wider.
A program may use at most 768 MiB of HBM per device.

v0:
```python
import jax
import jax.numpy as jnp
from jax import lax
from jax.sharding import PartitionSpec as P

EPSILON = 1e-5
NEG_BIG = -1e30


def rms_norm(residual, gain_vec):
    wide_res = residual.astype(jnp.float32)
    mean_sq = jnp.mean(wide_res * wide_res, axis=-1, keepdims=True)
    return (wide_res * lax.rsqrt(mean_sq + EPSILON) * gain_vec.astype(jnp.float32)).astype(jnp.bfloat16)


def local_attention(query_vec, k_layer, v_layer, valid_mask, score_scale):
    scores = jnp.einsum("bkgd,bktd->bkgt", query_vec, k_layer, preferred_element_type=jnp.float32) * score_scale
    scores = jnp.where(valid_mask, scores, NEG_BIG)
    local_max = jnp.max(scores, axis=-1)
    prob_w = jnp.where(valid_mask, jnp.exp(scores - local_max[..., None]), 0.0)
    local_sum = jnp.sum(prob_w, axis=-1)
    local_out = jnp.einsum("bkgt,bktd->bkgd", prob_w.astype(jnp.bfloat16), v_layer, preferred_element_type=jnp.float32)
    return jnp.concatenate([local_out, local_max[..., None], local_sum[..., None]], axis=-1)


def combine_parts(gathered, head_dim, new_score, val_new):
    part_out = gathered[..., :head_dim]
    part_max = gathered[..., head_dim]
    part_sum = gathered[..., head_dim + 1]
    run_max = jnp.maximum(jnp.max(part_max, axis=0), new_score)
    part_wt = jnp.exp(part_max - run_max)
    prob_new = jnp.exp(new_score - run_max)
    denom_sum = jnp.sum(part_wt * part_sum, axis=0) + prob_new
    numer_sum = jnp.sum(part_wt[..., None] * part_out, axis=0)
    numer_sum = numer_sum + prob_new.astype(jnp.bfloat16).astype(jnp.float32)[..., None] * val_new[:, :, None, :].astype(jnp.float32)
    return (numer_sum / denom_sum[..., None]).astype(jnp.bfloat16)


def solution(mesh):
    weight_col = P(None, None, "tp")
    weight_row = P(None, "tp", None)
    cache_spec = P(None, "dp", "tp", "sp", None)
    new_spec = P(None, "dp", "tp", None)

    def device_step(x_in, lengths, w_q, w_k, w_v, w_o, w_gate, w_up, w_down, gain_attn, gain_mlp, k_cache, v_cache):
        n_layers = w_q.shape[0]
        batch_size = x_in.shape[0]
        kv_heads = k_cache.shape[2]
        t_local = k_cache.shape[3]
        head_dim = k_cache.shape[4]
        q_heads = w_q.shape[2] // head_dim
        group_size = q_heads // kv_heads
        score_scale = head_dim ** -0.5
        positions = lax.axis_index("sp") * t_local + jnp.arange(t_local)
        valid_mask = (positions[None, :] < lengths[:, None])[:, None, None, :]
        residual = x_in
        key_list = []
        val_list = []
        for layer_idx in range(n_layers):
            normed = rms_norm(residual, gain_attn[layer_idx])
            query_vec = jnp.dot(normed, w_q[layer_idx], preferred_element_type=jnp.float32).astype(jnp.bfloat16).reshape(batch_size, kv_heads, group_size, head_dim)
            key_new = jnp.dot(normed, w_k[layer_idx], preferred_element_type=jnp.float32).astype(jnp.bfloat16).reshape(batch_size, kv_heads, head_dim)
            val_new = jnp.dot(normed, w_v[layer_idx], preferred_element_type=jnp.float32).astype(jnp.bfloat16).reshape(batch_size, kv_heads, head_dim)
            packed = local_attention(query_vec, k_cache[layer_idx], v_cache[layer_idx], valid_mask, score_scale)
            gathered = lax.all_gather(packed, "sp")
            new_score = jnp.einsum("clhe,cle->clh", query_vec, key_new, preferred_element_type=jnp.float32) * score_scale
            attn_out = combine_parts(gathered, head_dim, new_score, val_new).reshape(batch_size, q_heads * head_dim)
            attn_part = jnp.dot(attn_out, w_o[layer_idx], preferred_element_type=jnp.float32).astype(jnp.bfloat16)
            attn_sum = lax.psum(attn_part, "tp")
            residual = (residual.astype(jnp.float32) + attn_sum.astype(jnp.float32)).astype(jnp.bfloat16)
            normed_mlp = rms_norm(residual, gain_mlp[layer_idx])
            gate_proj = jnp.dot(normed_mlp, w_gate[layer_idx], preferred_element_type=jnp.float32)
            up_proj = jnp.dot(normed_mlp, w_up[layer_idx], preferred_element_type=jnp.float32)
            hidden_act = (jax.nn.silu(gate_proj) * up_proj).astype(jnp.bfloat16)
            mlp_part = jnp.dot(hidden_act, w_down[layer_idx], preferred_element_type=jnp.float32).astype(jnp.bfloat16)
            mlp_sum = lax.psum(mlp_part, "tp")
            residual = (residual.astype(jnp.float32) + mlp_sum.astype(jnp.float32)).astype(jnp.bfloat16)
            key_list.append(key_new)
            val_list.append(val_new)
        return residual, jnp.stack(key_list), jnp.stack(val_list)

    in_specs = (P("dp", None), P("dp"), weight_col, weight_col, weight_col, weight_row, weight_col, weight_col, weight_row, P(None, None), P(None, None), cache_spec, cache_spec)
    out_specs = (P("dp", None), new_spec, new_spec)
    return jax.shard_map(device_step, mesh=mesh, in_specs=in_specs, out_specs=out_specs, check_vma=False)
```

profile of v0, /device:TPU:97, one launch (start us, length us, event | category | flops | bytes accessed | tf_op | source)
XLA Modules:
  0.0 381.2 jit_solution(4123596126266826429)
XLA Ops:
  7.2 0.1 all-gather.5.cloned.1.call-start
  7.3 1.5 fusion.46
  8.8 0.8 slice_convert_fusion.3
  9.6 3.3 fusion.72
  13.0 0.1 broadcast_compare_fusion
  13.1 2.9 fusion.137
  15.9 0.4 fusion.102
  16.3 2.3 fusion.70
  18.6 0.9 copy.81
  19.5 0.9 copy.80
  20.4 0.2 pad_maximum_fusion
  20.6 0.9 copy.82
  21.6 0.1 all-reduce.5.cloned.1.call-start
  21.7 1.7 convolution_convert_fusion.4
  23.5 0.1 copy.83
  23.6 1.7 convolution_convert_fusion.5
  25.3 0.3 fusion.116
  25.6 0.1 copy.95
  25.7 21.3 %all-gather.5.cloned.1.call-done = f32[512,1,4,130]{0,2,3,1:T(4,128)} async-done(((f32[128,1,4,130]{0,2,3,1:T(4,128)}), f32[512,1,4,130]{0,2,3,1:T(4,128)}) %all-gather.5.cloned.1.call-update) | async-done | bytes 1064976 | tf_op jit(solution)/shard_map/all_gather | solution.py:65
  47.0 0.7 slice_reduce_fusion.1
  47.7 0.7 fusion.121
  48.4 0.7 exponential_bitcast_fusion.1
  49.1 1.6 fusion.79
  50.8 0.1 fusion.100
  50.9 3.9 %convolution_convert_fusion.1 = bf16[128,4096]{1,0:T(8,128)(2,1)} fusion(bf16[128,512]{0,1:T(8,128)(2,1)S(1)} %bitcast.189, bf16[2,512,4096]{2,1,0:T(8,128)(2,1)} %param.18), kind=kOutput, calls=%fused_computation.21 | convolution fusion | flops 537395200 | bytes 5373952 | tf_op jit(solution)/shard_map/dot_general | solution.py:68
  54.9 0.1 all-reduce.7.cloned.1.call-start
  55.0 57.6 %all-reduce.5.cloned.1.call-done = bf16[128,4096]{1,0:T(8,128)(2,1)} async-done(((bf16[128,4096]{1,0:T(8,128)(2,1)}), bf16[128,4096]{1,0:T(8,128)(2,1)}) %all-reduce.5.cloned.1.call-update) | async-done | bytes 1048592 | tf_op jit(solution)/shard_map/psum | solution.py:69
  112.6 1.7 fusion.50
  114.3 6.5 %fusion.10 = f32[128,1792]{1,0:T(8,128)S(1)} fusion(bf16[2,4096,1792]{2,1,0:T(8,128)(2,1)} %param.19, bf16[128,4096]{1,0:T(8,128)(2,1)S(1)} %get-tuple-element.6, f32[4096]{0:T(1024)S(1)} %bitcast.207, f32[128]{0:T(128)S(1)} %add_rsqrt_fusion.2), kind=kOutput, calls=%fused_computation.10 | convolution fusion | flops 1881145344 | bytes 16663040 | tf_op jit(solution)/shard_map/dot_general | solution.py:72
  120.8 12.9 %fusion.18 = bf16[128,4096]{1,0:T(8,128)(2,1)} fusion(bf16[2,1792,4096]{2,1,0:T(8,128)(2,1)} %param.21, bf16[2,4096,1792]{2,1,0:T(8,128)(2,1)} %param.20, f32[128,1792]{1,0:T(8,128)S(1)} %fusion.10, bf16[128,4096]{1,0:T(8,128)(2,1)S(1)} %get-tuple-element.6, f32[4096]{0:T(1024)S(1)} %bitcast.208, f32[128]{0:T(128)S(1)} %add_rsqrt_fusion.2), kind=kOutput, calls=%fused_computation.18 | convolution fusion | flops 3762094080 | bytes 32391680 | tf_op jit(solution)/shard_map/dot_general | solution.py:75
  133.8 0.2 all-gather.7.cloned.1.call-start
  134.0 56.6 %all-reduce.7.cloned.1.call-done = bf16[128,4096]{1,0:T(8,128)(2,1)} async-done(((bf16[128,4096]{1,0:T(8,128)(2,1)}), bf16[128,4096]{1,0:T(8,128)(2,1)}) %all-reduce.7.cloned.1.call-update) | async-done | bytes 1048592 | tf_op jit(solution)/shard_map/psum | solution.py:76
  190.6 1.7 fusion.54
  192.4 0.4 fusion.56
  192.8 1.0 copy-done.2
  193.8 2.9 fusion.75
  196.7 2.9 fusion.138
  199.6 0.4 fusion.104
  200.0 2.3 fusion.71
  202.3 0.9 copy.90
  203.2 0.9 copy.89
  204.1 0.2 pad_maximum_fusion.1
  204.3 0.9 copy.91
  205.3 0.1 all-reduce.9.cloned.1.call-start
  205.4 2.0 convolution_convert_fusion.3
  207.4 0.3 fusion.114
  207.7 0.1 copy.97
  207.8 1.7 convolution_convert_fusion.2
  209.5 0.1 copy.92
  209.6 18.6 %all-gather.7.cloned.1.call-done = f32[512,1,4,130]{0,2,3,1:T(4,128)} async-done(((f32[128,1,4,130]{0,2,3,1:T(4,128)}), f32[512,1,4,130]{0,2,3,1:T(4,128)}) %all-gather.7.cloned.1.call-update) | async-done | bytes 1064976 | tf_op jit(solution)/shard_map/all_gather | solution.py:65
  228.1 0.7 slice_reduce_fusion
  228.8 0.7 fusion.119
  229.6 0.7 exponential_bitcast_fusion
  230.3 1.6 fusion.78
  231.9 0.1 fusion.101
  232.0 3.9 %convolution_convert_fusion = bf16[128,4096]{1,0:T(8,128)(2,1)} fusion(bf16[128,512]{0,1:T(8,128)(2,1)S(1)} %bitcast.190, bf16[2,512,4096]{2,1,0:T(8,128)(2,1)} %param.18), kind=kOutput, calls=%fused_computation.20 | convolution fusion | flops 537395200 | bytes 5373952 | tf_op jit(solution)/shard_map/dot_general | solution.py:68
  236.0 0.1 all-reduce.11.cloned.1.call-start
  236.1 57.6 %all-reduce.9.cloned.1.call-done = bf16[128,4096]{1,0:T(8,128)(2,1)} async-done(((bf16[128,4096]{1,0:T(8,128)(2,1)}), bf16[128,4096]{1,0:T(8,128)(2,1)}) %all-reduce.9.cloned.1.call-update) | async-done | bytes 1048592 | tf_op jit(solution)/shard_map/psum | solution.py:69
  293.7 1.8 fusion.58
  295.6 6.5 %fusion.4 = f32[128,1792]{1,0:T(8,128)S(1)} fusion(bf16[2,4096,1792]{2,1,0:T(8,128)(2,1)} %param.19, bf16[128,4096]{1,0:T(8,128)(2,1)S(1)} %get-tuple-element.4, f32[4096]{0:T(1024)S(1)} %bitcast.202, f32[128]{0:T(128)S(1)} %add_rsqrt_fusion), kind=kOutput, calls=%fused_computation.4 | convolution fusion | flops 1881145344 | bytes 16663040 | tf_op jit(solution)/shard_map/dot_general | solution.py:72
  302.1 12.9 %fusion.21 = bf16[128,4096]{1,0:T(8,128)(2,1)} fusion(bf16[2,1792,4096]{2,1,0:T(8,128)(2,1)} %param.21, bf16[2,4096,1792]{2,1,0:T(8,128)(2,1)} %param.20, f32[128,1792]{1,0:T(8,128)S(1)} %fusion.4, bf16[128,4096]{1,0:T(8,128)(2,1)S(1)} %get-tuple-element.4, f32[4096]{0:T(1024)S(1)} %bitcast.203, f32[128]{0:T(128)S(1)} %add_rsqrt_fusion), kind=kOutput, calls=%fused_computation.19 | convolution fusion | flops 3762094080 | bytes 32391680 | tf_op jit(solution)/shard_map/dot_general | solution.py:75
  315.1 0.7 pad_maximum_fusion.2
  315.8 56.1 %all-reduce.11.cloned.1.call-done = bf16[128,4096]{1,0:T(8,128)(2,1)} async-done(((bf16[128,4096]{1,0:T(8,128)(2,1)}), bf16[128,4096]{1,0:T(8,128)(2,1)}) %all-reduce.11.cloned.1.call-update) | async-done | bytes 1048592 | tf_op jit(solution)/shard_map/psum | solution.py:76
  371.9 2.4 fusion.61
  (39 shorter events, 0.6 us)
Async XLA Ops:
  7.2 39.8 %all-gather.5.cloned.1.call-start = ((), (), s32[]{:S(2)}) async-start(), calls=%async_computation.4 | async-start | bytes 1331200 | tf_op jit(solution)/shard_map/all_gather | solution.py:65
  9.6 3.3 copy-start.9
  18.6 3.1 copy-start.1
  21.6 90.9 %all-reduce.5.cloned.1.call-start = ((), (), s32[]{:S(2)}) async-start(), calls=%async_computation | async-start | bytes 2097152 | tf_op jit(solution)/shard_map/psum | solution.py:69
  23.5 27.3 %copy-start.4 = (bf16[128,128]{1,0:T(8,128)(2,1)}, bf16[128,128]{1,0:T(8,128)(2,1)S(1)}, u32[]{:S(2)}) copy-start(bf16[128,128]{1,0:T(8,128)(2,1)S(1)} %convolution_convert_fusion.4) | copy-start | bytes 98308
  25.3 29.5 %copy-start.7 = (bf16[128,128]{1,0:T(8,128)(2,1)}, bf16[128,128]{1,0:T(8,128)(2,1)S(1)}, u32[]{:S(2)}) copy-start(bf16[128,128]{1,0:T(8,128)(2,1)S(1)} %convolution_convert_fusion.5) | copy-start | bytes 98308
  50.9 4.1 %copy-start.6 = (bf16[2,4096]{1,0:T(2,128)(2,1)S(1)}, bf16[2,4096]{1,0:T(2,128)(2,1)}, u32[]{:S(2)}) copy-start(bf16[2,4096]{1,0:T(2,128)(2,1)} %param.23) | copy-start | bytes 49156
  54.9 135.8 %all-reduce.7.cloned.1.call-start = ((), (), s32[]{:S(2)}) async-start(), calls=%async_computation.1 | async-start | bytes 2097152 | tf_op jit(solution)/shard_map/psum | solution.py:76
  133.8 94.3 %all-gather.7.cloned.1.call-start = ((), (), s32[]{:S(2)}) async-start(), calls=%async_computation.5 | async-start | bytes 1331200 | tf_op jit(solution)/shard_map/all_gather | solution.py:65
  190.6 1.7 copy-start
  192.8 1.0 copy-start.2
  205.3 2.5 copy-start.3
  205.3 88.4 %all-reduce.9.cloned.1.call-start = ((), (), s32[]{:S(2)}) async-start(), calls=%async_computation.2 | async-start | bytes 2097152 | tf_op jit(solution)/shard_map/psum | solution.py:69
  236.0 135.8 %all-reduce.11.cloned.1.call-start = ((), (), s32[]{:S(2)}) async-start(), calls=%async_computation.3 | async-start | bytes 2097152 | tf_op jit(solution)/shard_map/psum | solution.py:76
  302.1 13.0 %copy-start.5 = (bf16[128,128]{1,0:T(8,128)(2,1)S(1)}, bf16[128,128]{1,0:T(8,128)(2,1)}, u32[]{:S(2)}) copy-start(bf16[128,128]{1,0:T(8,128)(2,1)} %copy-done.4) | copy-start | bytes 98308
  302.1 13.0 %copy-start.8 = (bf16[128,128]{1,0:T(8,128)(2,1)S(1)}, bf16[128,128]{1,0:T(8,128)(2,1)}, u32[]{:S(2)}) copy-start(bf16[128,128]{1,0:T(8,128)(2,1)} %copy-done.7) | copy-start | bytes 98308
Sparse Core Ops, SparseCore 0:
  21.8 25.1 all-gather.4
  55.0 57.5 all-reduce.4
  133.9 56.6 all-reduce.6
  205.4 22.6 all-gather.6
  236.1 57.5 all-reduce.8
  315.2 56.6 all-reduce.10
where the time goes:
time: 383 us; the launch traced here: 381 us
  waiting for transfers between devices  268 us (70%)
  matrix products  70.9 us (19%)
  other arithmetic  20.2 us (5%)
  between operations  14.5 us (4%)
  local copies, waits for them, and re-layouts  6.9 us (2%)
    psum x2, waiting for transfers between devices, device_step(): attn_sum = lax.psum(attn_part, 'tp')  115 us
    psum x2, waiting for transfers between devices, device_step(): mlp_sum = lax.psum(mlp_part, 'tp')  113 us
    all_gather x2, waiting for transfers between devices, device_step(): gathered = lax.all_gather(packed, 'sp')  39.8 us
    dot_general x2, matrix products, device_step(): jnp.dot(hidden_act, w_down[layer_idx], preferred_element_type=jnp.float32)  25.8 us
    dot_general x2, matrix products, device_step(): jnp.dot(normed_mlp, w_gate[layer_idx], preferred_element_type=jnp.float32)  13 us
    dot_general x2, matrix products, device_step(): jnp.dot(attn_out, w_o[layer_idx], preferred_element_type=jnp.float32)  7.83 us
  transfers between devices with their start and end apart: 6, of which 6 were waited for; matrix products, arithmetic and copies ran while one was open for 2% of the time, Pallas kernels for 0%

commit v1 on v0

v1 whole, which is shorter than its diff:
```python
import functools

import jax
import jax.numpy as jnp
from jax import lax
from jax.experimental import pallas as pl
from jax.experimental.pallas import tpu as pltpu
from jax.sharding import PartitionSpec as P

EPSILON = 1e-5
NEG_BIG = -1e30
F32 = jnp.float32
BF16 = jnp.bfloat16
MESH = pl.DeviceIdType.MESH
VMEM_LIMIT = 67043328


def decode_kernel(
    n_sp, n_tp,
    len_ref, xin_hbm, wq_hbm, wk_hbm, wv_hbm, wo_hbm, wg_hbm, wu_hbm, wd_hbm, ga_ref, gm_ref, kc_hbm, vc_hbm,
    xo_ref, kn_ref, vn_ref,
    wqkv, wo, wg, wu, wd, kbuf, vbuf, xin, hrow, qkvf, qacc, snew, sbuf, obuf, stsend, orecv, strecv, o2d,
    gacc, uacc, act, psend, prev, precv, xres, xbuf,
    sem_x, sem_qkv, sem_wo, sem_wg, sem_wu, sem_wd, sem_kv,
    ys_send, ys_recv, yt_send, yt_recv, yq_send, yq_recv,
    rs_send, rs_recv, ag_send, ag_recv,
    f1_send, f1_recv, f2_send, f2_recv, f3_send, f3_recv,
):
    n_layers = wq_hbm.shape[0]
    batch, width = xin.shape
    head = kbuf.shape[1]
    qw = wq_hbm.shape[2]
    group = qw // head
    t_local = kbuf.shape[0] // batch
    rows = batch // n_sp
    cols = width // n_tp
    n_k = sem_qkv.shape[0]
    k_chunk = width // n_k
    n_gk = wg.shape[0]
    g_chunk = wg.shape[1]
    scale = head ** -0.5
    blk = rows * group
    sub = 16
    span = 4 * t_local
    s_idx = lax.axis_index("sp")
    i_idx = lax.axis_index("tp")

    def qkv_copies(l, c):
        ks = pl.ds(c * k_chunk, k_chunk)
        return (
            pltpu.make_async_copy(wq_hbm.at[l, ks, :], wqkv.at[ks, pl.ds(0, qw)], sem_qkv.at[c, 0]),
            pltpu.make_async_copy(wk_hbm.at[l, ks, :], wqkv.at[ks, pl.ds(qw, head)], sem_qkv.at[c, 1]),
            pltpu.make_async_copy(wv_hbm.at[l, ks, :], wqkv.at[ks, pl.ds(qw + head, head)], sem_qkv.at[c, 2]),
        )

    def wo_copy(l):
        return pltpu.make_async_copy(wo_hbm.at[l], wo, sem_wo)

    def wg_copy(l, c):
        return pltpu.make_async_copy(wg_hbm.at[l, pl.ds(c * g_chunk, g_chunk), :], wg.at[c], sem_wg.at[c])

    def wu_copy(l, c):
        return pltpu.make_async_copy(wu_hbm.at[l, pl.ds(c * g_chunk, g_chunk), :], wu.at[c], sem_wu.at[c])

    def wd_copy(l):
        return pltpu.make_async_copy(wd_hbm.at[l], wd, sem_wd)

    def kv_copies(l):
        return (
            pltpu.make_async_copy(kc_hbm.at[l], kbuf, sem_kv.at[0]),
            pltpu.make_async_copy(vc_hbm.at[l], vbuf, sem_kv.at[1]),
        )

    x_copy = pltpu.make_async_copy(xin_hbm, xin, sem_x)
    x_copy.start()
    for c in range(n_k):
        for cp in qkv_copies(0, c):
            cp.start()
    for cp in kv_copies(0):
        cp.start()
    wo_copy(0).start()
    for c in range(n_gk):
        wg_copy(0, c).start()
        wu_copy(0, c).start()
    wd_copy(0).start()

    barrier = pltpu.get_barrier_semaphore()
    for e in range(1, n_sp):
        pl.semaphore_signal(barrier, inc=1, device_id={"sp": lax.rem(s_idx + e, n_sp)}, device_id_type=MESH)
    for d in range(1, n_tp):
        pl.semaphore_signal(barrier, inc=1, device_id={"tp": lax.rem(i_idx + d, n_tp)}, device_id_type=MESH)

    def norm_block(load, store, gain_ref, l):
        total = None
        for c in range(n_tp):
            v = load(c).astype(F32)
            total = v * v if total is None else total + v * v
        mean_sq = jnp.sum(total, axis=-1, keepdims=True) * (1.0 / width)
        inv = lax.rsqrt(mean_sq + EPSILON)
        for c in range(n_tp):
            gain = gain_ref[pl.ds(l, 1), pl.ds(c * cols, cols)].astype(F32)
            store(c, (load(c).astype(F32) * inv * gain).astype(BF16))

    def project_qkv(l, h_ref, n_rows):
        qacc[pl.ds(0, n_rows), :] = jnp.zeros((n_rows, qacc.shape[1]), F32)

        @pl.loop(0, n_k)
        def _(c):
            for cp in qkv_copies(l, c):
                cp.wait()
            ks = pl.ds(pl.multiple_of(c * k_chunk, k_chunk), k_chunk)
            qacc[pl.ds(0, n_rows), :] += jnp.dot(h_ref[:, ks], wqkv[ks, :], preferred_element_type=F32)
            if l + 1 < n_layers:
                for cp in qkv_copies(l + 1, c):
                    cp.start()

    my_rows = pl.ds(pl.multiple_of(s_idx * rows, rows), rows)
    my_cols = pl.ds(pl.multiple_of(i_idx * cols, cols), cols)

    x_copy.wait()

    xres[...] = xin[my_rows, my_cols]

    @pl.loop(0, n_sp)
    def _(r):
        rs = pl.ds(pl.multiple_of(r * rows, rows), rows)

        def store(c, v):
            xin[rs, pl.ds(c * cols, cols)] = v

        norm_block(lambda c: xin[rs, pl.ds(c * cols, cols)], store, ga_ref, 0)

    pl.semaphore_wait(barrier, n_sp + n_tp - 2)

    def attention(l):
        qf = qkvf.at[l]
        for cp in kv_copies(l):
            cp.wait()

        @pl.loop(0, batch // sub)
        def _(gi):
            r0 = pl.multiple_of(gi * sub, sub)
            kk = qf[pl.ds(r0, sub), pl.ds(qw, head)].astype(F32)
            q64 = jnp.concatenate([qf[pl.ds(r0, sub), pl.ds(g * head, head)] for g in range(group)], axis=0)
            k16 = kbuf[pl.ds(pl.multiple_of(gi * sub * t_local, sub * t_local), sub * t_local), :]
            s4 = lax.dot_general(q64, k16, (((1,), (1,)), ((), ())), preferred_element_type=F32)
            which = lax.rem(lax.broadcasted_iota(jnp.int32, (group * sub, span), 0), sub) // 4
            comb = s4[:, 0:span]
            for j in range(1, sub // 4):
                comb = jnp.where(which == j, s4[:, j * span:(j + 1) * span], comb)
            o0 = pl.multiple_of(gi * group * sub, group * sub)
            sbuf[pl.ds(o0, group * sub), :] = comb * scale
            kt = jnp.concatenate([kk] * group, axis=0)
            snew[pl.ds(o0, group * sub), :] = jnp.sum(q64.astype(F32) * kt, axis=-1, keepdims=True) * scale

        @pl.loop(0, n_sp)
        def _(t):
            rs = pl.ds(pl.multiple_of(t * blk, blk), blk)
            row_b = lax.broadcasted_iota(jnp.int32, (blk, batch), 0)
            row_b = t * rows + (row_b // (group * sub)) * sub + lax.rem(row_b, sub)
            lane_b = lax.broadcasted_iota(jnp.int32, (blk, batch), 1)
            lens = len_ref[...].astype(F32)
            len_row = jnp.sum(jnp.where(row_b == lane_b, lens, 0.0), axis=1, keepdims=True)
            lane = lax.broadcasted_iota(jnp.int32, (blk, span), 1)
            row = lax.broadcasted_iota(jnp.int32, (blk, span), 0)
            pos = (lax.rem(lane, t_local) + s_idx * t_local).astype(F32)
            valid = jnp.logical_and(lane // t_local == lax.rem(row, 4), pos < len_row)
            sc = jnp.where(valid, sbuf[rs, :], NEG_BIG)
            top = jnp.maximum(jnp.max(sc, axis=-1, keepdims=True), snew[rs, :])
            prob = jnp.where(valid, jnp.exp(sc - top), 0.0)
            tot = jnp.sum(prob, axis=-1, keepdims=True)
            sbuf[rs, :] = prob
            eye = lax.broadcasted_iota(jnp.int32, (blk, blk), 0) == lax.broadcasted_iota(jnp.int32, (blk, blk), 1)
            stsend[t, pl.ds(0, 1), :] = jnp.sum(jnp.where(eye, top, 0.0), axis=0, keepdims=True)
            stsend[t, pl.ds(1, 1), :] = jnp.sum(jnp.where(eye, tot, 0.0), axis=0, keepdims=True)

        @pl.loop(0, batch // sub)
        def _(gi):
            o0 = pl.multiple_of(gi * group * sub, group * sub)
            pr = sbuf[pl.ds(o0, group * sub), :]
            which = lax.rem(lax.broadcasted_iota(jnp.int32, (group * sub, span), 0), sub) // 4
            wide = jnp.concatenate([jnp.where(which == j, pr, 0.0).astype(BF16) for j in range(sub // 4)], axis=1)
            v16 = vbuf[pl.ds(pl.multiple_of(gi * sub * t_local, sub * t_local), sub * t_local), :]
            obuf[pl.ds(o0, group * sub), :] = jnp.dot(wide, v16, preferred_element_type=F32).astype(BF16)

        if l + 1 < n_layers:
            for cp in kv_copies(l + 1):
                cp.start()

    def combine_over_sp(l):
        sends = []
        for e in range(1, n_sp):
            t = lax.rem(s_idx + e, n_sp)
            rs = pl.ds(pl.multiple_of(t * blk, blk), blk)
            a = pltpu.make_async_remote_copy(
                src_ref=stsend.at[t], dst_ref=strecv.at[e - 1], send_sem=yt_send.at[e - 1],
                recv_sem=yt_recv.at[e - 1], device_id={"sp": t}, device_id_type=MESH)
            b = pltpu.make_async_remote_copy(
                src_ref=obuf.at[rs, :], dst_ref=orecv.at[e - 1], send_sem=ys_send.at[e - 1],
                recv_sem=ys_recv.at[e - 1], device_id={"sp": t}, device_id_type=MESH)
            a.start()
            b.start()
            sends += [a, b]
        eye = lax.broadcasted_iota(jnp.int32, (blk, blk), 0) == lax.broadcasted_iota(jnp.int32, (blk, blk), 1)

        def column(v):
            return jnp.sum(jnp.where(eye, v, 0.0), axis=1, keepdims=True)

        my_blk = pl.ds(pl.multiple_of(s_idx * blk, blk), blk)
        sn = snew[my_blk, :]
        for cp in sends:
            cp.wait()
        tops = [column(stsend[s_idx, pl.ds(0, 1), :])] + [column(strecv[e, pl.ds(0, 1), :]) for e in range(n_sp - 1)]
        tots = [column(stsend[s_idx, pl.ds(1, 1), :])] + [column(strecv[e, pl.ds(1, 1), :]) for e in range(n_sp - 1)]
        run_max = sn
        for m in tops:
            run_max = jnp.maximum(run_max, m)
        p_new = jnp.exp(sn - run_max)
        denom = p_new
        v_own = qkvf[l, my_rows, pl.ds(qw + head, head)].astype(F32)
        v_rows = jnp.concatenate([v_own[b * sub:(b + 1) * sub] for b in range(rows // sub) for _ in range(group)], axis=0)
        numer = p_new.astype(BF16).astype(F32) * v_rows
        parts = [obuf[my_blk, :]] + [orecv[e] for e in range(n_sp - 1)]
        for m, tt, o in zip(tops, tots, parts):
            w = jnp.exp(m - run_max)
            denom = denom + w * tt
            numer = numer + w * o.astype(F32)
        res = (numer / denom).astype(BF16)
        for b in range(rows // sub):
            for g in range(group):
                a0 = (b * group + g) * sub
                o2d[pl.ds(b * sub, sub), pl.ds(g * head, head)] = res[a0:a0 + sub, :]

    def rs_copy(d, j):
        return pltpu.make_async_remote_copy(
            src_ref=psend.at[d], dst_ref=precv.at[d], send_sem=rs_send.at[d], recv_sem=rs_recv.at[d],
            device_id={"tp": j}, device_id_type=MESH)

    def reduce_over_tp(lhs_ref, w_ref, step):
        @pl.loop(0, n_tp // step)
        def _(it):
            for u in range(step):
                d = it * step + u
                j = lax.rem(i_idx + 1 + d, n_tp)
                part = jnp.dot(lhs_ref[...], w_ref[:, pl.ds(pl.multiple_of(j * cols, cols), cols)],
                               preferred_element_type=F32)
                if u < step - 1:
                    psend[d] = part.astype(BF16)
                    rs_copy(d, j).start()
                else:
                    @pl.when(d < n_tp - 1)
                    def _():
                        psend[d] = part.astype(BF16)
                        rs_copy(d, j).start()

                    @pl.when(d == n_tp - 1)
                    def _():
                        prev[...] = part

        acc = prev[...]
        for d in range(n_tp - 1):
            rs_copy(d, lax.rem(i_idx + 1 + d, n_tp)).wait()
            acc = acc + precv[d].astype(F32)
        xres[...] = (xres[...].astype(F32) + acc).astype(BF16)

    def ag_copy(d):
        return pltpu.make_async_remote_copy(
            src_ref=xres, dst_ref=xbuf.at[i_idx], send_sem=ag_send.at[d], recv_sem=ag_recv.at[d],
            device_id={"tp": lax.rem(i_idx + 1 + d, n_tp)}, device_id_type=MESH)

    def gather_and_norm(gain_ref, l):
        for d in range(n_tp - 1):
            ag_copy(d).start()
        xbuf[i_idx] = xres[...]
        for d in range(n_tp - 1):
            ag_copy(d).wait()

        def store(c, v):
            hrow[:, pl.ds(c * cols, cols)] = v

        norm_block(lambda c: xbuf[c], store, gain_ref, l)

    for l in range(n_layers):
        if l == 0:
            project_qkv(l, xin, batch)
            qkvf[l] = qacc[...].astype(BF16)
        else:
            gather_and_norm(ga_ref, l)
            project_qkv(l, hrow, rows)
            qkvf[l, my_rows, :] = qacc[pl.ds(0, rows), :].astype(BF16)
            copies = []
            for e in range(1, n_sp):
                cp = pltpu.make_async_remote_copy(
                    src_ref=qkvf.at[l, my_rows, :], dst_ref=qkvf.at[l, my_rows, :], send_sem=yq_send.at[e - 1],
                    recv_sem=yq_recv.at[e - 1], device_id={"sp": lax.rem(s_idx + e, n_sp)}, device_id_type=MESH)
                cp.start()
                copies.append(cp)
            for cp in copies:
                cp.wait()
        kn_ref[l] = qkvf[l, :, pl.ds(qw, head)]
        vn_ref[l] = qkvf[l, :, pl.ds(qw + head, head)]
        attention(l)
        combine_over_sp(l)
        wo_copy(l).wait()
        reduce_over_tp(o2d, wo, n_tp // 2)
        if l + 1 < n_layers:
            wo_copy(l + 1).start()
        gather_and_norm(gm_ref, l)
        gacc[...] = jnp.zeros(gacc.shape, F32)
        uacc[...] = jnp.zeros(uacc.shape, F32)

        @pl.loop(0, n_gk)
        def _(c):
            wg_copy(l, c).wait()
            wu_copy(l, c).wait()
            hk = hrow[:, pl.ds(pl.multiple_of(c * g_chunk, g_chunk), g_chunk)]
            gacc[...] += jnp.dot(hk, wg[c], preferred_element_type=F32)
            uacc[...] += jnp.dot(hk, wu[c], preferred_element_type=F32)
            if l + 1 < n_layers:
                wg_copy(l + 1, c).start()
                wu_copy(l + 1, c).start()

        act[...] = (jax.nn.silu(gacc[...]) * uacc[...]).astype(BF16)
        wd_copy(l).wait()
        reduce_over_tp(act, wd, 2)
        if l + 1 < n_layers:
            wd_copy(l + 1).start()

    xo_ref[my_rows, my_cols] = xres[...]
    f1 = []
    for e in range(1, n_sp):
        cp = pltpu.make_async_remote_copy(
            src_ref=xres, dst_ref=xo_ref.at[my_rows, my_cols], send_sem=f1_send.at[e - 1], recv_sem=f1_recv.at[e - 1],
            device_id={"sp": lax.rem(s_idx + e, n_sp)}, device_id_type=MESH)
        cp.start()
        f1.append(cp)
    for cp in f1:
        cp.wait()

    def strip(j):
        return xo_ref.at[:, pl.ds(pl.multiple_of(j * cols, cols), cols)]

    f2 = []
    for d in range(1, n_tp // 2):
        cp = pltpu.make_async_remote_copy(
            src_ref=strip(i_idx), dst_ref=strip(i_idx), send_sem=f2_send.at[d - 1], recv_sem=f2_recv.at[d - 1],
            device_id={"tp": lax.rem(i_idx + 2 * d, n_tp)}, device_id_type=MESH)
        cp.start()
        f2.append(cp)
    partner = i_idx + 1 - 2 * lax.rem(i_idx, 2)
    f3 = []
    for d in range(n_tp // 2):
        if d > 0:
            f2[d - 1].wait()
        j = lax.rem(i_idx + n_tp - 2 * d, n_tp)
        cp = pltpu.make_async_remote_copy(
            src_ref=strip(j), dst_ref=strip(j), send_sem=f3_send.at[d], recv_sem=f3_recv.at[d],
            device_id={"tp": partner}, device_id_type=MESH)
        cp.start()
        f3.append(cp)
    for cp in f3:
        cp.wait()


def solution(mesh):
    weight_col = P(None, None, "tp")
    weight_row = P(None, "tp", None)
    cache_spec = P(None, "dp", "tp", "sp", None)
    new_spec = P(None, "dp", "tp", None)
    n_sp = mesh.shape["sp"]
    n_tp = mesh.shape["tp"]

    def device_step(x_in, lengths, w_q, w_k, w_v, w_o, w_gate, w_up, w_down, gain_attn, gain_mlp, k_cache, v_cache):
        n_layers, width, qw = w_q.shape
        batch = x_in.shape[0]
        t_local, head = k_cache.shape[3], k_cache.shape[4]
        ff = w_gate.shape[2]
        group = qw // head
        rows, cols = batch // n_sp, width // n_tp
        n_k, n_gk = 4, 4
        kc = k_cache.reshape(n_layers, batch * t_local, head)
        vc = v_cache.reshape(n_layers, batch * t_local, head)
        vm = pl.BlockSpec(memory_space=pltpu.VMEM)
        hbm = pl.BlockSpec(memory_space=pl.ANY)
        dma = pltpu.SemaphoreType.DMA
        scratch = [
            pltpu.VMEM((width, qw + 2 * head), BF16),
            pltpu.VMEM((qw, width), BF16),
            pltpu.VMEM((n_gk, width // n_gk, ff), BF16),
            pltpu.VMEM((n_gk, width // n_gk, ff), BF16),
            pltpu.VMEM((ff, width), BF16),
            pltpu.VMEM((batch * t_local, head), BF16),
            pltpu.VMEM((batch * t_local, head), BF16),
            pltpu.VMEM((batch, width), BF16),
            pltpu.VMEM((rows, width), BF16),
            pltpu.VMEM((n_layers, batch, qw + 2 * head), BF16),
            pltpu.VMEM((batch, qw + 2 * head), F32),
            pltpu.VMEM((batch * group, 1), F32),
            pltpu.VMEM((batch * group, 4 * t_local), F32),
            pltpu.VMEM((batch * group, head), BF16),
            pltpu.VMEM((n_sp, 8, rows * group), F32),
            pltpu.VMEM((n_sp - 1, rows * group, head), BF16),
            pltpu.VMEM((n_sp - 1, 8, rows * group), F32),
            pltpu.VMEM((rows, qw), BF16),
            pltpu.VMEM((rows, ff), F32),
            pltpu.VMEM((rows, ff), F32),
            pltpu.VMEM((rows, ff), BF16),
            pltpu.VMEM((n_tp - 1, rows, cols), BF16),
            pltpu.VMEM((rows, cols), F32),
            pltpu.VMEM((n_tp - 1, rows, cols), BF16),
            pltpu.VMEM((rows, cols), BF16),
            pltpu.VMEM((n_tp, rows, cols), BF16),
            dma, dma((n_k, 3)), dma, dma((n_gk,)), dma((n_gk,)), dma, dma((2,)),
        ]
        scratch += [dma((n_sp - 1,))] * 6 + [dma((n_tp - 1,))] * 4
        scratch += [dma((n_sp - 1,))] * 2 + [dma((n_tp // 2 - 1,))] * 2 + [dma((n_tp // 2,))] * 2
        x_out, k_new, v_new = pl.pallas_call(
            functools.partial(decode_kernel, n_sp, n_tp),
            out_shape=(
                jax.ShapeDtypeStruct((batch, width), BF16),
                jax.ShapeDtypeStruct((n_layers, batch, head), BF16),
                jax.ShapeDtypeStruct((n_layers, batch, head), BF16),
            ),
            in_specs=[vm, hbm, hbm, hbm, hbm, hbm, hbm, hbm, hbm, vm, vm, hbm, hbm],
            out_specs=(vm, vm, vm),
            scratch_shapes=scratch,
            compiler_params=pltpu.CompilerParams(collective_id=0, has_side_effects=True, vmem_limit_bytes=VMEM_LIMIT),
            name="decode_layers",
        )(lengths.reshape(1, batch), x_in, w_q, w_k, w_v, w_o, w_gate, w_up, w_down, gain_attn, gain_mlp, kc, vc)
        return x_out, k_new.reshape(n_layers, batch, 1, head), v_new.reshape(n_layers, batch, 1, head)

    in_specs = (P("dp", None), P("dp"), weight_col, weight_col, weight_col, weight_row, weight_col, weight_col, weight_row, P(None, None), P(None, None), cache_spec, cache_spec)
    out_specs = (P("dp", None), new_spec, new_spec)
    return jax.shard_map(device_step, mesh=mesh, in_specs=in_specs, out_specs=out_specs, check_vma=False)
```

time: 383 us -> 113 us (0.30)
  waiting for transfers between devices: 268 us -> 0 us
  Pallas kernels: 0 us -> 107 us
  matrix products: 70.9 us -> 0 us
  other arithmetic: 20.2 us -> 0 us
  between operations: 14.5 us -> 0.65 us
    psum x4 -> x0, waiting for transfers between devices: 228 us -> none  [the longest x2 115 us: device_step(): attn_sum = lax.psum(attn_part, 'tp')]
    pallas_call x0 -> x1, Pallas kernels: none -> 107 us  [device_step(): pl.pallas_call(functools.partial(decode_kernel, n_sp, n_tp), out_shape=(j...]
    dot_general x18 -> x0, matrix products: 70.9 us -> none  [the longest x2 25.8 us: device_step(): jnp.dot(hidden_act, w_down[layer_idx], preferred_element_type=jnp.float32)]
    all_gather x2 -> x0, waiting for transfers between devices: 39.8 us -> none  [device_step(): gathered = lax.all_gather(packed, 'sp')]
    reduce_sum x10 -> x0, other arithmetic: 12.3 us -> none  [the longest x4 6.74 us: rms_norm(): mean_sq = jnp.mean(wide_res * wide_res, axis=-1, keepdims=True)]
    unnamed x20 -> x3, local copies, waits for them, and re-layouts: 1.01 us -> 5.23 us
  transfers between devices with their start and end apart: 6 -> 0, of which waited for: 6 -> 0; matrix products, arithmetic and copies ran while one was open for 2% -> 0% of each run, Pallas kernels for 0% -> 0%
where the time goes in v1:
time: 113 us
  Pallas kernels  107 us (95%)
  local copies, waits for them, and re-layouts  5.23 us (5%)
    pallas_call x1, Pallas kernels, device_step(): pl.pallas_call(functools.partial(decode_kernel, n_sp, n_tp), out_shape=(j...  107 us
    unnamed x3, local copies, waits for them, and re-layouts  5.23 us

profile of v1, /device:TPU:97, one launch (start us, length us, event | category | flops | bytes accessed | tf_op | source)
XLA Modules:
  0.0 113.0 jit_solution(16296641405261888856)
XLA Ops:
  0.6 107.2 %decode_layers.1 = (bf16[128,4096]{1,0:T(8,128)(2,1)}, bf16[2,128,128]{2,1,0:T(8,128)(2,1)}, bf16[2,128,128]{2,1,0:T(8,128)(2,1)}) custom-call(s32[1,128]{1,0:T(1,128)} %bitcast.13, bf16[128,4096]{1,0:T(8,128)(2,1)} %xin_hbm.1, bf16[2,4096,512]{2,1,0:T(8,128)(2,1)} %wq_hbm.1, bf16[2,4096,128]{2,1,0:T(8,128)(2,1)} %wk_hbm.1, bf16[2,4096,128]{2,1,0:T(8,128)(2,1)} %wv_hbm.1, ...), custom_call_target="tpu_custom_call" | custom-call | tf_op jit(solution)/shard_map/decode_layers/pallas_call | solution.py:417
  107.8 2.3 %copy.21 = bf16[128,4096]{1,0:T(8,128)(2,1)} copy(bf16[128,4096]{1,0:T(8,128)(2,1)} %get-tuple-element.15) | data formatting | bytes 2097152
  110.1 1.5 %copy.22 = bf16[2,128,1,128]{3,1,2,0:T(8,128)(2,1)} copy(bf16[2,128,1,128]{3,1,2,0:T(8,128)(2,1)} %bitcast.12) | data formatting | bytes 131072
  111.6 1.5 %copy.23 = bf16[2,128,1,128]{3,1,2,0:T(8,128)(2,1)} copy(bf16[2,128,1,128]{3,1,2,0:T(8,128)(2,1)} %bitcast.11) | data formatting | bytes 131072

commit v2 on v1

v2 whole, which is shorter than its diff:
```python
import functools
import itertools

import jax
import jax.numpy as jnp
from jax import lax
from jax.experimental import pallas as pl
from jax.experimental.pallas import tpu as pltpu
from jax.sharding import PartitionSpec as P

EPSILON = 1e-5
NEG_BIG = -1e30
F32 = jnp.float32
BF16 = jnp.bfloat16
MESH = pl.DeviceIdType.MESH
VMEM_LIMIT = 64487424


def decode_kernel(
    n_sp, n_tp,
    len_ref, xin_hbm, wq_hbm, wk_hbm, wv_hbm, wo_hbm, wg_hbm, wu_hbm, wd_hbm, ga_ref, gm_ref, kc_hbm, vc_hbm,
    xo_ref, kn_ref, vn_ref,
    wqkv, wo, wg, wu, wd, kbuf, vbuf, xin, hrow, qkvf, qacc, snew, obuf, stsend, orecv, strecv, o2d,
    gacc, uacc, act, psend, prev, precv, xres, xbuf,
    sem_x, sem_qkv, sem_wo, sem_wg, sem_wu, sem_wd, sem_kv,
    ys_send, ys_recv, yt_send, yt_recv, yq_send, yq_recv,
    rs_send, rs_recv, ag_send, ag_recv,
    f1_send, f1_recv, f2_send, f2_recv, f3_send, f3_recv,
):
    scope = jax.named_scope
    n_layers = wq_hbm.shape[0]
    batch, width = xin.shape
    head = kbuf.shape[1]
    qw = wq_hbm.shape[2]
    group = qw // head
    t_local = kbuf.shape[0] // batch
    rows = batch // n_sp
    cols = width // n_tp
    n_k = sem_qkv.shape[0]
    k_chunk = width // n_k
    n_gk = wg.shape[0]
    g_chunk = wg.shape[1]
    scale = head ** -0.5
    blk = rows * group
    sub = 16
    span = 4 * t_local
    s_idx = lax.axis_index("sp")
    i_idx = lax.axis_index("tp")

    def tp_peer(d):
        return lax.rem(i_idx + tp_offset(d), n_tp)

    def tp_offset(d):
        turn = (d + 1) // 2
        return (n_tp // 2 + turn - 2 * turn * (d % 2)) % n_tp

    def qkv_copies(l, c):
        ks = pl.ds(c * k_chunk, k_chunk)
        return (
            pltpu.make_async_copy(wq_hbm.at[l, ks, :], wqkv.at[ks, pl.ds(0, qw)], sem_qkv.at[c, 0]),
            pltpu.make_async_copy(wk_hbm.at[l, ks, :], wqkv.at[ks, pl.ds(qw, head)], sem_qkv.at[c, 1]),
            pltpu.make_async_copy(wv_hbm.at[l, ks, :], wqkv.at[ks, pl.ds(qw + head, head)], sem_qkv.at[c, 2]),
        )

    def wo_copy(l):
        return pltpu.make_async_copy(wo_hbm.at[l], wo, sem_wo)

    def wg_copy(l, c):
        return pltpu.make_async_copy(wg_hbm.at[l, pl.ds(c * g_chunk, g_chunk), :], wg.at[c], sem_wg.at[c])

    def wu_copy(l, c):
        return pltpu.make_async_copy(wu_hbm.at[l, pl.ds(c * g_chunk, g_chunk), :], wu.at[c], sem_wu.at[c])

    def wd_copy(l):
        return pltpu.make_async_copy(wd_hbm.at[l], wd, sem_wd)

    def kv_copies(l):
        return (
            pltpu.make_async_copy(kc_hbm.at[l], kbuf, sem_kv.at[0]),
            pltpu.make_async_copy(vc_hbm.at[l], vbuf, sem_kv.at[1]),
        )

    x_copy = pltpu.make_async_copy(xin_hbm, xin, sem_x)
    x_copy.start()

    barrier = pltpu.get_barrier_semaphore()
    for e in range(1, n_sp):
        pl.semaphore_signal(barrier, inc=1, device_id={"sp": lax.rem(s_idx + e, n_sp)}, device_id_type=MESH)
    for d in range(1, n_tp):
        pl.semaphore_signal(barrier, inc=1, device_id={"tp": lax.rem(i_idx + d, n_tp)}, device_id_type=MESH)

    def norm_block(load, store, gain_ref, l):
        total = None
        for c in range(n_tp):
            v = load(c).astype(F32)
            total = v * v if total is None else total + v * v
        mean_sq = jnp.sum(total, axis=-1, keepdims=True) * (1.0 / width)
        inv = lax.rsqrt(mean_sq + EPSILON)
        for c in range(n_tp):
            gain = gain_ref[pl.ds(l, 1), pl.ds(c * cols, cols)].astype(F32)
            store(c, (load(c).astype(F32) * inv * gain).astype(BF16))

    def project_qkv(l, h_ref, n_rows):
        qacc[pl.ds(0, n_rows), :] = jnp.zeros((n_rows, qacc.shape[1]), F32)

        @pl.loop(0, n_k)
        def _(c):
            for cp in qkv_copies(l, c):
                cp.wait()
            ks = pl.ds(pl.multiple_of(c * k_chunk, k_chunk), k_chunk)
            qacc[pl.ds(0, n_rows), :] += jnp.dot(h_ref[:, ks], wqkv[ks, :], preferred_element_type=F32)
            if l + 1 < n_layers:
                for cp in qkv_copies(l + 1, c):
                    cp.start()

    my_rows = pl.ds(pl.multiple_of(s_idx * rows, rows), rows)
    my_cols = pl.ds(pl.multiple_of(i_idx * cols, cols), cols)

    with scope("x_wait"):
        x_copy.wait()
    for c in range(n_k):
        for cp in qkv_copies(0, c):
            cp.start()
    for cp in kv_copies(0):
        cp.start()
    wo_copy(0).start()

    xres[...] = xin[my_rows, my_cols]

    with scope("norm"):
        @pl.loop(0, n_sp)
        def _(r):
            rs = pl.ds(pl.multiple_of(r * rows, rows), rows)

            def store(c, v):
                xin[rs, pl.ds(c * cols, cols)] = v

            norm_block(lambda c: xin[rs, pl.ds(c * cols, cols)], store, ga_ref, 0)


    def sp_copies(e):
        t = lax.rem(s_idx + e, n_sp)
        return (
            pltpu.make_async_remote_copy(
                src_ref=stsend.at[t], dst_ref=strecv.at[e - 1], send_sem=yt_send.at[e - 1],
                recv_sem=yt_recv.at[e - 1], device_id={"sp": t}, device_id_type=MESH),
            pltpu.make_async_remote_copy(
                src_ref=obuf.at[t], dst_ref=orecv.at[e - 1], send_sem=ys_send.at[e - 1],
                recv_sem=ys_recv.at[e - 1], device_id={"sp": t}, device_id_type=MESH),
        )

    def qkv_copy(l, e):
        return pltpu.make_async_remote_copy(
            src_ref=qkvf.at[l, my_rows, :], dst_ref=qkvf.at[l, my_rows, :], send_sem=yq_send.at[e - 1],
            recv_sem=yq_recv.at[e - 1], device_id={"sp": lax.rem(s_idx + e, n_sp)}, device_id_type=MESH)

    n_sub = rows // sub
    tall = group * sub
    which = lax.rem(lax.broadcasted_iota(jnp.int32, (tall, span), 0), sub) // 4
    eye = lax.broadcasted_iota(jnp.int32, (blk, blk), 0) == lax.broadcasted_iota(jnp.int32, (blk, blk), 1)

    def attend(l, t):
        scores, news = [], []
        for u in range(n_sub):
            r0 = pl.multiple_of(t * rows + u * sub, sub)
            kk = qkvf[l, pl.ds(r0, sub), pl.ds(qw, head)].astype(F32)
            q64 = jnp.concatenate([qkvf[l, pl.ds(r0, sub), pl.ds(g * head, head)] for g in range(group)], axis=0)
            k16 = kbuf[pl.ds(pl.multiple_of(r0 * t_local, sub * t_local), sub * t_local), :]
            s4 = lax.dot_general(q64, k16, (((1,), (1,)), ((), ())), preferred_element_type=F32)
            comb = s4[:, 0:span]
            for j in range(1, sub // 4):
                comb = jnp.where(which == j, s4[:, j * span:(j + 1) * span], comb)
            scores.append(comb * scale)
            kt = jnp.concatenate([kk] * group, axis=0)
            news.append(jnp.sum(q64.astype(F32) * kt, axis=-1, keepdims=True) * scale)
        score = jnp.concatenate(scores, axis=0)
        s_new = jnp.concatenate(news, axis=0)
        row_b = lax.broadcasted_iota(jnp.int32, (blk, batch), 0)
        row_b = t * rows + (row_b // tall) * sub + lax.rem(row_b, sub)
        lane_b = lax.broadcasted_iota(jnp.int32, (blk, batch), 1)
        lens = len_ref[...].astype(F32)
        len_row = jnp.sum(jnp.where(row_b == lane_b, lens, 0.0), axis=1, keepdims=True)
        lane = lax.broadcasted_iota(jnp.int32, (blk, span), 1)
        row = lax.broadcasted_iota(jnp.int32, (blk, span), 0)
        pos = (lax.rem(lane, t_local) + s_idx * t_local).astype(F32)
        valid = jnp.logical_and(lane // t_local == lax.rem(row, 4), pos < len_row)
        score = jnp.where(valid, score, NEG_BIG)
        top = jnp.maximum(jnp.max(score, axis=-1, keepdims=True), s_new)
        prob = jnp.where(valid, jnp.exp(score - top), 0.0)
        tot = jnp.sum(prob, axis=-1, keepdims=True)
        stsend[t, pl.ds(0, 1), :] = jnp.sum(jnp.where(eye, top, 0.0), axis=0, keepdims=True)
        stsend[t, pl.ds(1, 1), :] = jnp.sum(jnp.where(eye, tot, 0.0), axis=0, keepdims=True)
        for u in range(n_sub):
            pr = prob[u * tall:(u + 1) * tall]
            wide = jnp.concatenate([jnp.where(which == j, pr, 0.0).astype(BF16) for j in range(sub // 4)], axis=1)
            v0 = pl.multiple_of((t * rows + u * sub) * t_local, sub * t_local)
            obuf[t, pl.ds(u * tall, tall), :] = jnp.dot(
                wide, vbuf[pl.ds(v0, sub * t_local), :], preferred_element_type=F32).astype(BF16)
        return s_new

    def attention(l):
        for cp in kv_copies(l):
            cp.wait()
        order = (2, 1, 3, 0) if l == 0 else (0, 1, 3, 2)
        for e in order:
            if l > 0 and e > 0:
                qkv_copy(l, n_sp - e).wait()
            out = attend(l, lax.rem(s_idx + e, n_sp))
            if l == 0 and e == order[0]:
                pl.semaphore_wait(barrier, n_sp + n_tp - 2)
            if e == 0:
                snew[...] = out
            else:
                for cp in sp_copies(e):
                    cp.start()
        if l + 1 < n_layers:
            for cp in kv_copies(l + 1):
                cp.start()

    def combine_over_sp(l):
        def column(v):
            return jnp.sum(jnp.where(eye, v, 0.0), axis=1, keepdims=True)

        sn = snew[...]
        tops = [column(stsend[s_idx, pl.ds(0, 1), :])]
        tots = [column(stsend[s_idx, pl.ds(1, 1), :])]
        parts = [obuf[s_idx]]
        with scope("sp_wait"):
            for e in range(1, n_sp):
                for cp in sp_copies(e):
                    cp.wait()
        for e in range(1, n_sp):
            tops.append(column(strecv[e - 1, pl.ds(0, 1), :]))
            tots.append(column(strecv[e - 1, pl.ds(1, 1), :]))
            parts.append(orecv[e - 1])
        run_max = sn
        for m in tops:
            run_max = jnp.maximum(run_max, m)
        p_new = jnp.exp(sn - run_max)
        denom = p_new
        v_own = qkvf[l, my_rows, pl.ds(qw + head, head)].astype(F32)
        v_rows = jnp.concatenate([v_own[b * sub:(b + 1) * sub] for b in range(n_sub) for _ in range(group)], axis=0)
        numer = p_new.astype(BF16).astype(F32) * v_rows
        for m, tt, o in zip(tops, tots, parts):
            w = jnp.exp(m - run_max)
            denom = denom + w * tt
            numer = numer + w * o.astype(F32)
        res = (numer / denom).astype(BF16)
        for b in range(n_sub):
            for g in range(group):
                a0 = (b * group + g) * sub
                o2d[pl.ds(b * sub, sub), pl.ds(g * head, head)] = res[a0:a0 + sub, :]

    def rs_copy(d, j):
        return pltpu.make_async_remote_copy(
            src_ref=psend.at[d], dst_ref=precv.at[d], send_sem=rs_send.at[d], recv_sem=rs_recv.at[d],
            device_id={"tp": j}, device_id_type=MESH)

    def reduce_over_tp(lhs_ref, w_ref, step):
        @pl.loop(0, n_tp // step)
        def _(it):
            for u in range(step):
                d = it * step + u
                j = tp_peer(d)
                part = jnp.dot(lhs_ref[...], w_ref[:, pl.ds(pl.multiple_of(j * cols, cols), cols)],
                               preferred_element_type=F32)
                if u < step - 1:
                    psend[d] = part.astype(BF16)
                    rs_copy(d, j).start()
                else:
                    @pl.when(d < n_tp - 1)
                    def _():
                        psend[d] = part.astype(BF16)
                        rs_copy(d, j).start()

                    @pl.when(d == n_tp - 1)
                    def _():
                        prev[...] = part

        with scope("reduce"):
            acc = prev[...]
            for d in range(n_tp - 1):
                rs_copy(d, tp_peer(d)).wait()
                acc = acc + precv[d].astype(F32)
        xres[...] = (xres[...].astype(F32) + acc).astype(BF16)

    def ag_copy(d):
        return pltpu.make_async_remote_copy(
            src_ref=xres, dst_ref=xbuf.at[i_idx], send_sem=ag_send.at[d], recv_sem=ag_recv.at[d],
            device_id={"tp": tp_peer(d)}, device_id_type=MESH)

    def gather_and_norm(gain_ref, l):
        for d in range(n_tp - 1):
            ag_copy(d).start()
        xbuf[i_idx] = xres[...]
        for d in range(n_tp - 1):
            ag_copy(d).wait()

        def store(c, v):
            hrow[:, pl.ds(c * cols, cols)] = v

        with scope("norm"):
            norm_block(lambda c: xbuf[c], store, gain_ref, l)

    for l in range(n_layers):
        if l == 0:
            with scope("qkv"):
                project_qkv(l, xin, batch)
                qkvf[l] = qacc[...].astype(BF16)
            for c in range(n_gk):
                wg_copy(0, c).start()
                wu_copy(0, c).start()
        else:
            with scope("gather_a"):
                gather_and_norm(ga_ref, l)
            with scope("qkv"):
                project_qkv(l, hrow, rows)
                qkvf[l, my_rows, :] = qacc[pl.ds(0, rows), :].astype(BF16)
            for e in (2, 1, 3):
                qkv_copy(l, e).start()
        with scope("attention"):
            attention(l)
        kn_ref[l] = qkvf[l, :, pl.ds(qw, head)]
        vn_ref[l] = qkvf[l, :, pl.ds(qw + head, head)]
        if l == 0:
            wd_copy(0).start()
        with scope("combine"):
            combine_over_sp(l)
        with scope("wo"):
            wo_copy(l).wait()
            reduce_over_tp(o2d, wo, n_tp // 2)
        if l + 1 < n_layers:
            wo_copy(l + 1).start()
        with scope("gather_m"):
            gather_and_norm(gm_ref, l)
        with scope("gate_up"):
            gacc[...] = jnp.zeros(gacc.shape, F32)
            uacc[...] = jnp.zeros(uacc.shape, F32)

            @pl.loop(0, n_gk)
            def _(c):
                wg_copy(l, c).wait()
                wu_copy(l, c).wait()
                hk = hrow[:, pl.ds(pl.multiple_of(c * g_chunk, g_chunk), g_chunk)]
                gacc[...] += jnp.dot(hk, wg[c], preferred_element_type=F32)
                uacc[...] += jnp.dot(hk, wu[c], preferred_element_type=F32)
                if l + 1 < n_layers:
                    wg_copy(l + 1, c).start()
                    wu_copy(l + 1, c).start()

            act[...] = (jax.nn.silu(gacc[...]) * uacc[...]).astype(BF16)
        with scope("down"):
            wd_copy(l).wait()
            reduce_over_tp(act, wd, 2)
        if l + 1 < n_layers:
            wd_copy(l + 1).start()

    n_x = n_tp // 2
    half = rows // 2
    partner = i_idx + 1 - 2 * lax.rem(i_idx, 2)

    def block(e, d, r0, n):
        t = lax.rem(s_idx + n_sp - e, n_sp)
        j = lax.rem(i_idx + n_tp - 2 * d, n_tp)
        return xo_ref.at[pl.ds(pl.multiple_of(t * rows + r0, half), n), pl.ds(pl.multiple_of(j * cols, cols), cols)]

    def send_sp(ref, e, k):
        return pltpu.make_async_remote_copy(
            src_ref=ref, dst_ref=ref, send_sem=f1_send.at[k], recv_sem=f1_recv.at[k],
            device_id={"sp": lax.rem(s_idx + e, n_sp)}, device_id_type=MESH)

    def send_x(ref, d, k):
        return pltpu.make_async_remote_copy(
            src_ref=ref, dst_ref=ref, send_sem=f2_send.at[k], recv_sem=f2_recv.at[k],
            device_id={"tp": lax.rem(i_idx + 2 * d, n_tp)}, device_id_type=MESH)

    def send_core(ref, k):
        return pltpu.make_async_remote_copy(
            src_ref=ref, dst_ref=ref, send_sem=f3_send.at[k], recv_sem=f3_recv.at[k],
            device_id={"tp": partner}, device_id_type=MESH)

    sent = []

    def go(cp):
        cp.start()
        sent.append(cp)

    with scope("final"):
        xo_ref[my_rows, my_cols] = xres[...]
        far_sp = sorted(range(1, n_sp), key=lambda e: -min(e, n_sp - e))
        far_x = sorted(range(1, n_x), key=lambda d: -min(d, n_x - d))
        for e, d in itertools.zip_longest(far_sp, far_x):
            if e is not None:
                go(send_sp(block(0, 0, 0, rows), e, e - 1))
            if d is not None:
                go(send_x(block(0, 0, 0, rows), d, d - 1))
        core = []

        def to_core(ref):
            cp = send_core(ref, len(core))
            core.append(cp)
            go(cp)

        to_core(block(0, 0, 0, rows))
        for e, d in itertools.zip_longest(far_sp[::-1], far_x[::-1]):
            if e is not None:
                ref = block(e, 0, 0, rows)
                send_sp(ref, e, e - 1).wait_recv()
                for d2 in far_x:
                    go(send_x(block(e, 0, 0, half), d2, (n_x - 1) * e + d2 - 1))
                to_core(ref)
            if d is not None:
                ref = block(0, d, 0, rows)
                send_x(ref, d, d - 1).wait_recv()
                for e2 in far_sp:
                    go(send_sp(block(0, d, half, half), e2, (n_sp - 1) * d + e2 - 1))
                to_core(ref)
        for e in far_sp[::-1]:
            for d in far_x[::-1]:
                ref = block(e, d, 0, half)
                send_x(ref, d, (n_x - 1) * e + d - 1).wait_recv()
                to_core(ref)
                ref = block(e, d, half, half)
                send_sp(ref, e, (n_sp - 1) * d + e - 1).wait_recv()
                to_core(ref)
        for cp in core:
            cp.wait_recv()
        for cp in sent:
            cp.wait_send()


def solution(mesh):
    weight_col = P(None, None, "tp")
    weight_row = P(None, "tp", None)
    cache_spec = P(None, "dp", "tp", "sp", None)
    new_spec = P(None, "dp", "tp", None)
    n_sp = mesh.shape["sp"]
    n_tp = mesh.shape["tp"]

    def device_step(x_in, lengths, w_q, w_k, w_v, w_o, w_gate, w_up, w_down, gain_attn, gain_mlp, k_cache, v_cache):
        n_layers, width, qw = w_q.shape
        batch = x_in.shape[0]
        t_local, head = k_cache.shape[3], k_cache.shape[4]
        ff = w_gate.shape[2]
        group = qw // head
        rows, cols = batch // n_sp, width // n_tp
        n_k, n_gk = 4, 4
        kc = k_cache.reshape(n_layers, batch * t_local, head)
        vc = v_cache.reshape(n_layers, batch * t_local, head)
        vm = pl.BlockSpec(memory_space=pltpu.VMEM)
        hbm = pl.BlockSpec(memory_space=pl.ANY)
        dma = pltpu.SemaphoreType.DMA
        scratch = [
            pltpu.VMEM((width, qw + 2 * head), BF16),
            pltpu.VMEM((qw, width), BF16),
            pltpu.VMEM((n_gk, width // n_gk, ff), BF16),
            pltpu.VMEM((n_gk, width // n_gk, ff), BF16),
            pltpu.VMEM((ff, width), BF16),
            pltpu.VMEM((batch * t_local, head), BF16),
            pltpu.VMEM((batch * t_local, head), BF16),
            pltpu.VMEM((batch, width), BF16),
            pltpu.VMEM((rows, width), BF16),
            pltpu.VMEM((n_layers, batch, qw + 2 * head), BF16),
            pltpu.VMEM((batch, qw + 2 * head), F32),
            pltpu.VMEM((rows * group, 1), F32),
            pltpu.VMEM((n_sp, rows * group, head), BF16),
            pltpu.VMEM((n_sp, 8, rows * group), F32),
            pltpu.VMEM((n_sp - 1, rows * group, head), BF16),
            pltpu.VMEM((n_sp - 1, 8, rows * group), F32),
            pltpu.VMEM((rows, qw), BF16),
            pltpu.VMEM((rows, ff), F32),
            pltpu.VMEM((rows, ff), F32),
            pltpu.VMEM((rows, ff), BF16),
            pltpu.VMEM((n_tp - 1, rows, cols), BF16),
            pltpu.VMEM((rows, cols), F32),
            pltpu.VMEM((n_tp - 1, rows, cols), BF16),
            pltpu.VMEM((rows, cols), BF16),
            pltpu.VMEM((n_tp, rows, cols), BF16),
            dma, dma((n_k, 3)), dma, dma((n_gk,)), dma((n_gk,)), dma, dma((2,)),
        ]
        scratch += [dma((n_sp - 1,))] * 6 + [dma((n_tp - 1,))] * 4
        n_x = n_tp // 2
        scratch += [dma(((n_sp - 1) * n_x,))] * 2 + [dma(((n_x - 1) * n_sp,))] * 2 + [dma((2 * n_sp * n_x - n_sp - n_x + 1,))] * 2
        x_out, k_new, v_new = pl.pallas_call(
            functools.partial(decode_kernel, n_sp, n_tp),
            out_shape=(
                pltpu.VMEM((batch, width), BF16),
                pltpu.VMEM((n_layers, batch, head), BF16),
                pltpu.VMEM((n_layers, batch, head), BF16),
            ),
            in_specs=[vm, hbm, hbm, hbm, hbm, hbm, hbm, hbm, hbm, vm, vm, hbm, hbm],
            out_specs=(vm, vm, vm),
            scratch_shapes=scratch,
            compiler_params=pltpu.CompilerParams(collective_id=0, has_side_effects=True, vmem_limit_bytes=VMEM_LIMIT),
            name="decode_layers",
        )(lengths.reshape(1, batch), x_in, w_q, w_k, w_v, w_o, w_gate, w_up, w_down, gain_attn, gain_mlp, kc, vc)
        return x_out, k_new.reshape(n_layers, batch, 1, head), v_new.reshape(n_layers, batch, 1, head)

    in_specs = (P("dp", None), P("dp"), weight_col, weight_col, weight_col, weight_row, weight_col, weight_col, weight_row, P(None, None), P(None, None), cache_spec, cache_spec)
    out_specs = (P("dp", None), new_spec, new_spec)
    return jax.shard_map(device_step, mesh=mesh, in_specs=in_specs, out_specs=out_specs, check_vma=False)
```

time: 113 us -> 90.2 us (0.80)
  Pallas kernels: 107 us -> 87.1 us
  local copies, waits for them, and re-layouts: 5.23 us -> 2.23 us
    pallas_call x1, Pallas kernels: 107 us -> 87.1 us  [device_step(): pl.pallas_call(functools.partial(decode_kernel, n_sp, n_tp), out_shape=(p...]
    unnamed x3, local copies, waits for them, and re-layouts: 5.23 us -> 2.23 us
where the time goes in v2:
time: 90.2 us; the launch traced here: 90 us
  Pallas kernels  87.1 us (97%)
  local copies, waits for them, and re-layouts  2.23 us (2%)
    pallas_call x1, Pallas kernels, device_step(): pl.pallas_call(functools.partial(decode_kernel, n_sp, n_tp), out_shape=(p...  87.1 us
    unnamed x3, local copies, waits for them, and re-layouts  2.23 us

profile of v2, /device:TPU:97, one launch (start us, length us, event | category | flops | bytes accessed | tf_op | source)
XLA Modules:
  0.0 90.0 jit_solution(15017591279665920463)
XLA Ops:
  0.6 87.1 %decode_layers.1 = (bf16[128,4096]{1,0:T(8,128)(2,1)S(1)}, bf16[2,128,128]{2,1,0:T(8,128)(2,1)S(1)}, bf16[2,128,128]{2,1,0:T(8,128)(2,1)S(1)}) custom-call(s32[1,128]{1,0:T(1,128)} %bitcast.13, bf16[128,4096]{1,0:T(8,128)(2,1)} %xin_hbm.1, bf16[2,4096,512]{2,1,0:T(8,128)(2,1)} %wq_hbm.1, bf16[2,4096,128]{2,1,0:T(8,128)(2,1)} %wk_hbm.1, ...), custom_call_target="tpu_custom_call" | custom-call | tf_op jit(solution)/shard_map/decode_layers/pallas_call | solution.py:484
  87.7 1.0 %copy.21 = bf16[128,4096]{1,0:T(8,128)(2,1)} copy(bf16[128,4096]{1,0:T(8,128)(2,1)S(1)} %get-tuple-element.12) | data formatting | bytes 2097152
  88.7 0.6 copy.22
  89.3 0.6 copy.23
